TPU v7x, 128 devices: a whole 4x4x4 slice. The times are simulated.
128 devices in a mesh: sub: 8 (over z, core), ma: 16 (over y, x).
Axes of the slice: x: 4, y: 4, z: 4, core: 2. Of those that a mesh axis runs over, the one named last changes fastest.
Arguments:
- forcing: float32 [2, 512, 2, 128, 512], P(None, 'sub', None, 'ma'), may hold values from -24 to 24
- slot_wavenumber: int32 [128], P('ma'), may hold values from 0 to 511, as said below
- inverse: float32 [8, 2, 64, 64, 512], P('sub'), may hold values from -2 to 2
- edge_weights: float32 [8, 2, 64], P('sub'), may hold values from -2908 to 2908, as said below
Outputs:
- transform_field: float32 [2, 512, 2, 128, 512], P(None, ('sub', 'ma'))
Inputs may be any that keep to these rules, and one draw needn't show every extreme that they name: `slot_wavenumber`: each device's slots hold 4 pairs: slots 2j and 2j + 1 carry a wavenumber m below 256 and 511 - m, in that order; no wavenumber appears twice. `edge_weights`: together with inverse it makes every row of the interface system strictly diagonally dominant with a positive diagonal.
All inputs are finite; a program needn't handle non-finite values.
Results may differ from a plain program's by a relative error of at most 0.0003.
Values sent between devices are 32-bit elements; how exact they have to be, the bound alone decides.
A program may use at most 192 MiB of HBM per device.

v0:
```python
import math

import jax
import jax.numpy as jnp
from jax import lax
from jax.sharding import PartitionSpec as P

HIGH = lax.Precision.HIGHEST


def sent_to_all(shard, axis):
    copies = jnp.broadcast_to(shard, (lax.axis_size(axis), *shard.shape))
    return lax.all_to_all(copies, axis, split_axis=0, concat_axis=0, tiled=True)


def laid_out(tiles, dim):
    dims = list(tiles.shape[1:])
    dims[dim] *= tiles.shape[0]
    return jnp.moveaxis(tiles, 0, dim).reshape(dims)


def gather_directly(shard, axis, dim):
    tiles = sent_to_all(shard, axis)
    return laid_out(tiles, dim)


def in_one_piece(arrays, axis, dim, along):
    widths = [math.prod(a.shape[along:]) for a in arrays]
    both = jnp.concatenate(
        [a.reshape(*a.shape[:along], w) for a, w in zip(arrays, widths)], axis=along
    )
    out = gather_directly(both, axis, dim)
    tiles = jnp.split(out, [sum(widths[:k]) for k in range(1, len(widths))], axis=along)
    return tuple((b.reshape(*out.shape[:along], *a.shape[along:]) for a, b in zip(arrays, tiles)))


def widen(values):
    return values[:, None, None, :]


def body(forcing, slot_wavenumber, inverse, edge_weights):
    fields, points, halves, slot_count, degrees = forcing.shape
    block_inverse = inverse[0]
    edge_rows = edge_weights[0]
    degree = jnp.arange(degrees, dtype=jnp.int32)
    kept_modes = (degree[None, :] >= slot_wavenumber[:, None]).astype(jnp.float32)
    position = jnp.arange(points, dtype=jnp.int32)
    interior = ((position > 0) & (position < points - 1)).astype(jnp.float32)
    source = forcing * kept_modes[None, None, None, :, :] * interior[None, :, None, None, None]
    particular = jnp.einsum("fpql,fqcml->fpcml", block_inverse, source, precision=HIGH)
    low_slope = jnp.einsum("p,fpcml->fcml", edge_rows[0], particular, precision=HIGH)
    top_slope = jnp.einsum("p,fpcml->fcml", edge_rows[1], particular, precision=HIGH)
    lower_unit = block_inverse[:, :, 0, :]
    upper_unit = block_inverse[:, :, points - 1, :]
    low_influence = jnp.stack(
        [
            jnp.einsum("p,fpl->fl", edge_rows[0], lower_unit, precision=HIGH),
            jnp.einsum("p,fpl->fl", edge_rows[0], upper_unit, precision=HIGH),
        ]
    )
    top_influence = jnp.stack(
        [
            jnp.einsum("p,fpl->fl", edge_rows[1], lower_unit, precision=HIGH),
            jnp.einsum("p,fpl->fl", edge_rows[1], upper_unit, precision=HIGH),
        ]
    )
    sub_index = lax.axis_index("sub")
    gathered = in_one_piece(
        (top_slope[None], top_influence[None], low_slope[None], low_influence[None]), "sub", 0, 3
    )
    all_top_slope, all_top_influence, all_low_slope, all_low_influence = gathered
    lower_coefs = all_top_influence[:-1, 0]
    middle_coefs = all_top_influence[:-1, 1] - all_low_influence[1:, 0]
    upper_coefs = -all_low_influence[1:, 1]
    right_sides = all_low_slope[1:] - all_top_slope[:-1]

    def eliminate(state_pair, inputs):
        ratio_prev, reduced_prev = state_pair
        lower_here, middle_here, upper_here, right_here = inputs
        pivot_value = middle_here - lower_here * ratio_prev
        ratio_here = upper_here / pivot_value
        reduced_here = (right_here - widen(lower_here) * reduced_prev) / widen(pivot_value)
        return ((ratio_here, reduced_here), (ratio_here, reduced_here))

    initial = (jnp.zeros_like(lower_coefs[0]), jnp.zeros_like(right_sides[0]))
    _, (ratios, reduceds) = lax.scan(
        eliminate, initial, (lower_coefs, middle_coefs, upper_coefs, right_sides)
    )

    def substitute(later_value, inputs):
        ratio_here, reduced_here = inputs
        current = reduced_here - widen(ratio_here) * later_value
        return (current, current)

    _, interface = lax.scan(
        substitute, jnp.zeros_like(right_sides[0]), (ratios, reduceds), reverse=True
    )
    boundary = jnp.zeros_like(interface[:1])
    lower_value = lax.dynamic_index_in_dim(
        jnp.concatenate([boundary, interface]), sub_index, 0, keepdims=False
    )
    upper_value = lax.dynamic_index_in_dim(
        jnp.concatenate([interface, boundary]), sub_index, 0, keepdims=False
    )
    solution = particular + lower_value[:, None] * lower_unit[:, :, None, None, :]
    solution = solution + upper_value[:, None] * upper_unit[:, :, None, None, :]
    return lax.all_to_all(solution, "ma", split_axis=1, concat_axis=3, tiled=True)


def solution(mesh):
    return jax.shard_map(
        body,
        mesh=mesh,
        in_specs=(
            P(None, "sub", None, "ma", None),
            P("ma"),
            P("sub", None, None, None, None),
            P("sub", None, None),
        ),
        out_specs=P(None, ("sub", "ma"), None, None, None),
        check_vma=False,
    )
```

profile of v0, /device:TPU:1, one launch (start us, length us, event | category | flops | bytes accessed | tf_op | source)
XLA Modules:
  0.0 233.1 jit_solution(1013579382292759196)
XLA Ops:
  0.0 2.7 %fusion.34 = (f32[2,64,1,512]{3,2,1,0:T(1,128)S(1)}, f32[2,64,1,512]{3,2,1,0:T(1,128)S(1)}) fusion(f32[2,64,64,512]{3,2,1,0:T(8,128)} %bitcast.121), kind=kLoop, calls=%fused_computation.59 | loop fusion | bytes 1048576 | tf_op jit(solution)/shard_map/slice | solution.py:53
  2.8 0.9 fusion.4
  3.7 0.9 fusion.2
  4.6 0.9 fusion.8
  5.5 0.9 fusion.6
  6.4 0.7 fusion.18
  7.2 4.6 %multiply_multiply_fusion = f32[2,64,2,8,512]{4,3,2,1,0:T(8,128)} fusion(f32[2,64,2,8,512]{4,3,2,1,0:T(8,128)} %param.8, f32[64]{0:T(128)S(1)} %and_convert_fusion, f32[8,512]{1,0:T(8,128)S(1)} %fusion.18), kind=kLoop, calls=%fused_computation.16 | loop fusion | flops 2097152 | bytes 8405248 | tf_op jit(solution)/shard_map/mul | solution.py:49
  11.8 8.7 %copy.30 = f32[2,64,2,8,512]{1,3,2,4,0:T(8,128)} copy(f32[2,64,2,8,512]{4,3,2,1,0:T(8,128)} %multiply_multiply_fusion) | data formatting | bytes 8388608 | tf_op jit(solution)/shard_map/mul | solution.py:49
  20.4 30.5 %copy.40 = f32[2,64,64,512,1]{2,1,4,3,0:T(8,128)} copy(f32[2,64,64,512,1]{3,2,1,0,4:T(8,128)} %bitcast.122) | data formatting | bytes 33554432 | tf_op jit(solution)/shard_map/squeeze | solution.py:43
  51.0 57.6 %fusion.35 = f32[2,512,2,8,64]{4,3,2,1,0:T(8,128)} fusion(f32[2,64,2,8,512]{1,3,2,4,0:T(8,128)} %copy.30, f32[2,64,64,512,1]{2,1,4,3,0:T(8,128)} %copy.40), kind=kOutput, calls=%fused_computation.60 | convolution fusion | flops 805306368 | bytes 25165824 | tf_op jit(solution)/shard_map/fpql,fqcml->fpcml/dot_general | solution.py:50
  108.6 0.0 copy-start
  108.6 7.6 %copy.32 = f32[2,2,8,512,64]{3,2,4,1,0:T(8,128)} copy(f32[2,2,8,512,64]{4,2,1,3,0:T(8,128)} %bitcast.120) | data formatting | bytes 8388608 | tf_op jit(solution)/shard_map/p,fpcml->fcml/dot_general | solution.py:52
  116.2 5.0 %reshape.63 = f32[2,2,4096,64]{2,3,1,0:T(8,128)} reshape(f32[2,2,8,512,64]{3,2,4,1,0:T(8,128)} %copy.32) | data formatting | bytes 8388608 | tf_op jit(solution)/shard_map/reshape.50
  121.2 0.0 copy-done
  121.2 4.5 %fusion.21 = f32[1,2,2,4096]{3,0,2,1:T(1,128)S(1)} fusion(f32[2,2,4096,64]{2,3,1,0:T(8,128)} %reshape.63, f32[1,2,64]{2,1,0:T(2,128)S(1)} %copy-done), kind=kOutput, calls=%fused_computation.47 | convolution fusion | flops 12582912 | bytes 4260352 | tf_op jit(solution)/shard_map/p,fpcml->fcml/dot_general | solution.py:51
  125.6 4.5 %fusion.25 = f32[1,2,2,4096]{3,0,2,1:T(1,128)S(1)} fusion(f32[2,2,4096,64]{2,3,1,0:T(8,128)} %reshape.63, f32[1,2,64]{2,1,0:T(2,128)S(1)} %copy-done), kind=kOutput, calls=%fused_computation.51 | convolution fusion | flops 12582912 | bytes 4260352 | tf_op jit(solution)/shard_map/p,fpcml->fcml/dot_general | solution.py:52
  130.1 0.1 copy.46
  130.2 0.1 copy.42
  130.3 0.1 maximum_bitcast_fusion
  130.4 1.3 broadcast_in_dim.46
  131.7 6.8 %all-to-all-start = ((f32[8,1,2,2,9216]{4,3,2,1,0:T(2,128)}), f32[8,1,2,2,9216]{4,3,2,1,0:T(2,128)S(1)}, u32[]{:S(2)}, u32[]{:S(2)}) async-start(f32[8,1,2,2,9216]{4,3,2,1,0:T(2,128)} %broadcast_in_dim.46), calls=%async_computation | async-start | bytes 2359296 | tf_op jit(solution)/shard_map/all_to_all | solution.py:13
  138.5 0.2 copy.55
  138.7 0.2 copy.54
  138.9 15.9 %all-to-all-done = f32[8,1,2,2,9216]{4,3,2,1,0:T(2,128)S(1)} async-done(((f32[8,1,2,2,9216]{4,3,2,1,0:T(2,128)}), f32[8,1,2,2,9216]{4,3,2,1,0:T(2,128)S(1)}, u32[]{:S(2)}, u32[]{:S(2)}) %all-to-all-start) | async-done | bytes 1179680 | tf_op jit(solution)/shard_map/all_to_all | solution.py:13
  154.9 0.2 slice_subtract_fusion
  155.1 0.4 sub.37
  155.6 0.5 while.34
  156.2 0.5 while.35
  156.7 0.5 copy.35
  157.3 0.5 copy.33
  157.8 8.6 %fusion.1 = f32[2,64,2,8,512]{1,3,2,4,0:T(8,128)} fusion(f32[2,512,2,8,64]{4,3,2,1,0:T(8,128)} %fusion.35, f32[2,64,512]{1,2,0:T(8,128)S(1)} %bitcast.126, f32[2,2,8,512]{2,1,3,0:T(2,128)S(1)} %copy.35, f32[2,64,512]{1,2,0:T(8,128)S(1)} %bitcast.127, f32[2,2,8,512]{2,1,3,0:T(2,128)S(1)} %copy.33), kind=kLoop, calls=%fused_computation.14 | loop fusion | flops 4194304 | bytes 9043968 | tf_op jit(solution)/shard_map/add | solution.py:106
  166.4 7.6 %copy.37 = f32[2,64,2,8,512]{4,3,2,0,1:T(8,128)} copy(f32[2,64,2,8,512]{1,3,2,4,0:T(8,128)} %fusion.1) | data formatting | bytes 8388608 | tf_op jit(solution)/shard_map/add | solution.py:106
  174.0 56.5 %all_to_all.23 = f32[2,64,2,8,512]{4,3,2,0,1:T(8,128)S(1)} all-to-all(f32[2,64,2,8,512]{4,3,2,0,1:T(8,128)} %copy.37), channel_id=1, replica_groups=mesh['sub'=8,'ma'=16] {'ma'}, dimensions={1} | all-to-all | bytes 8388608 | tf_op jit(solution)/shard_map/all_to_all | solution.py:107
  230.5 2.7 %copy.73 = f32[2,4,2,16,8,512]{5,4,3,2,1,0:T(8,128)} copy(f32[2,4,2,16,8,512]{5,4,2,0,1,3:T(8,128)S(1)} %bitcast.123) | data formatting | bytes 8388608 | tf_op jit(solution)/shard_map/all_to_all | solution.py:107
  (42 shorter events, 0.8 us)
Async XLA Ops:
  108.6 12.6 %copy-start = (f32[1,2,64]{2,1,0:T(2,128)S(1)}, f32[1,2,64]{2,1,0:T(2,128)}, u32[]{:S(2)}) copy-start(f32[1,2,64]{2,1,0:T(2,128)} %param.11) | copy-start | bytes 1540
  131.7 23.2 %all-to-all-start = ((f32[8,1,2,2,9216]{4,3,2,1,0:T(2,128)}), f32[8,1,2,2,9216]{4,3,2,1,0:T(2,128)S(1)}, u32[]{:S(2)}, u32[]{:S(2)}) async-start(f32[8,1,2,2,9216]{4,3,2,1,0:T(2,128)} %broadcast_in_dim.46), calls=%async_computation | async-start | bytes 2359296 | tf_op jit(solution)/shard_map/all_to_all | solution.py:13
where the time goes:
time: 235 us; the launch traced here: 233 us
  matrix products  70.3 us (30%)
  local copies, waits for them, and re-layouts  68.2 us (29%)
  blocking collectives  56.5 us (24%)
  waiting for transfers between devices  15.9 us (7%)
  other arithmetic  14.9 us (6%)
  starting transfers between devices  6.8 us (3%)
    dot_general x1, matrix products, body(): jnp.einsum('fpql,fqcml->fpcml', block_inverse, source, precision=HIGH)  57.6 us
    all_to_all x1, blocking collectives, body(): lax.all_to_all(solution, 'ma', split_axis=1, concat_axis=3, tiled=True)  56.5 us
    squeeze x1, local copies, waits for them, and re-layouts, body(): block_inverse = inverse[0]  30.5 us
    all_to_all x1, waiting for transfers between devices, sent_to_all(): return lax.all_to_all(copies, axis, split_axis=0, concat_axis=0, tiled=True)  15.9 us
    mul x1, local copies, waits for them, and re-layouts, body(): forcing * kept_modes[None, None, None, :, :]  8.66 us
    add x1, other arithmetic, body(): solution = solution + upper_value[:, None] * upper_unit[:, :, None, None, :]  8.58 us
    dot_general x2, local copies, waits for them, and re-layouts, body(): jnp.einsum('p,fpcml->fcml', edge_rows[1], particular, precision=HIGH)  7.68 us
    add x1, local copies, waits for them, and re-layouts, body(): solution = solution + upper_value[:, None] * upper_unit[:, :, None, None, :]  7.61 us
  transfers between devices with their start and end apart: 1, of which 1 were waited for; matrix products, arithmetic and copies ran while one was open for 0% of the time, Pallas kernels for 0%

commit v1 on v0

v1 whole, which is shorter than its diff:
```python
import functools

import jax
import jax.numpy as jnp
from jax import lax
from jax.experimental import pallas as pl
from jax.experimental.pallas import tpu as pltpu
from jax.sharding import PartitionSpec as P

MESH = pl.DeviceIdType.MESH
F32 = jnp.float32
NP = 64
NS = 8
NM = 16
TILES = (2, 1, 3, 0)
STEPS = tuple((f, t) for f in range(2) for t in TILES)
NSTEP = len(STEPS)
PB = 8
QB = 16


def has_odd(k):
    return STEPS[k][1] >= 2


def odd_index(k):
    return STEPS[k][0] * 2 + STEPS[k][1] - 2


def iota(dim):
    return lax.broadcasted_iota(jnp.int32, (8, 128), dim)


def row(ref, *at):
    return jnp.broadcast_to(ref[at], (8, 128))


def flip_lanes(x):
    return jnp.take_along_axis(x, 127 - iota(1), axis=1)


def solve_kernel(
    forcing, slots, edges, inverse, packed, extras, modes,
    inv, raw, even, odd, even_part, odd_part, odd_flip, sent, weights, slopes, values, lasts, last_rows, own_modes,
    inv_sem, raw_sem, slope_send, slope_recv, field_send, field_recv, last_send, last_recv, mode_send, mode_recv,
):
    sub = lax.axis_index("sub")
    me = lax.axis_index("ma")
    y, x = me // 4, lax.rem(me, 4)
    subs = [lax.rem(sub + d, NS) for d in range(1, NS)]
    peers = []
    for dy in (2, 1, 3, 0):
        for dx in (2, 1, 3, 0):
            if dy or dx:
                peers.append(lax.rem(y + dy, 4) * 4 + lax.rem(x + dx, 4))

    barrier = pltpu.get_barrier_semaphore()
    for other in subs:
        pl.semaphore_signal(barrier, inc=1, device_id={"sub": other}, device_id_type=MESH)
    for other in peers:
        pl.semaphore_signal(barrier, inc=1, device_id={"ma": other}, device_id_type=MESH)

    def load(k):
        f, t = STEPS[k]
        lanes = pl.ds(t * 128, 128)
        return (
            pltpu.make_async_copy(inverse.at[f, :, :, lanes], inv.at[k], inv_sem.at[k]),
            pltpu.make_async_copy(forcing.at[f, :, :, lanes], raw.at[k], raw_sem.at[k]),
        )

    def start_load(k):
        for copy in load(k):
            copy.start()

    for k in range(3):
        start_load(k)

    pair = lax.rem(iota(0), 4)
    even_mode = jnp.zeros((8, 128), jnp.int32)
    odd_mode = jnp.zeros((8, 128), jnp.int32)
    for j in range(4):
        even_mode = jnp.where(pair == j, slots[2 * j], even_mode)
        odd_mode = jnp.where(pair == j, slots[2 * j + 1], odd_mode)
    own_modes[...] = even_mode.astype(F32)
    lane = iota(1)

    def slope_step(k):
        f, t = STEPS[k]
        for copy in load(k):
            copy.wait()
        if k + 3 < NSTEP:
            start_load(k + 3)
        even_kept = lane + t * 128 >= even_mode
        odd_kept = lane + t * 128 >= odd_mode
        zero = jnp.zeros((8, 128), F32)
        o = odd_index(k)

        def prepare(b, _):
            for i in range(8):
                q = b * 8 + i
                even[k, q] = jnp.where(even_kept, raw[k, q, pl.ds(0, 8, stride=2), :], zero)
                if has_odd(k):
                    odd[o, q] = jnp.where(odd_kept, raw[k, q, pl.ds(1, 8, stride=2), :], zero)
            return 0

        lax.fori_loop(0, NP // 8, prepare, 0)
        for q in (0, NP - 1):
            even[k, q] = zero
            if has_odd(k):
                odd[o, q] = zero

        def weigh(b, _):
            rows = pl.ds(pl.multiple_of(b * 8, 8), 8)
            low = [zero] * 2
            top = [zero] * 2
            for p in range(NP):
                block = inv[k, p, rows, :]
                low[p % 2] = low[p % 2] + edges[0, 0, p] * block
                top[p % 2] = top[p % 2] + edges[0, 1, p] * block
            weights[0, rows, :] = low[0] + low[1]
            weights[1, rows, :] = top[0] + top[1]
            return 0

        lax.fori_loop(0, NP // 8, weigh, 0)

        def gather(b, sums):
            sums = list(sums)
            for i in range(8):
                q = b * 8 + i
                for e in range(2):
                    weight = row(weights, e, pl.ds(q, 1), slice(None))
                    sums[e] = sums[e] + weight * even[k, q]
                    if has_odd(k):
                        sums[2 + e] = sums[2 + e] + weight * odd[o, q]
            return tuple(sums)

        sums = lax.fori_loop(0, NP // 8, gather, (zero,) * (4 if has_odd(k) else 2))
        for e in range(2):
            slopes[k, sub, e] = sums[e]
            for i, q in enumerate((0, NP - 1)):
                slopes[k, sub, 2, 2 * e + i : 2 * e + i + 1, :] = weights[e, q : q + 1, :]
            if has_odd(k):
                slopes[k, sub, 3 + e] = sums[2 + e]

    def slope_copies(k):
        count = 5 if has_odd(k) else 3
        here = slopes.at[k, sub, pl.ds(0, count)]
        return [
            pltpu.make_async_remote_copy(
                here, here, slope_send.at[k, i], slope_recv.at[k, i],
                device_id={"sub": other}, device_id_type=MESH,
            )
            for i, other in enumerate(subs)
        ]

    def particular_step(k):
        o = odd_index(k)
        both = has_odd(k)
        zero = jnp.zeros((8, 128), F32)

        def block(b, _):
            def inner(c, sums):
                sums = list(sums)
                for i in range(QB):
                    q = c * QB + i
                    source = even[k, q]
                    other = odd[o, q] if both else None
                    for j in range(PB):
                        weight = row(inv, k, b * PB + j, pl.ds(q, 1), slice(None))
                        sums[j] = sums[j] + weight * source
                        if both:
                            sums[PB + j] = sums[PB + j] + weight * other
                return tuple(sums)

            sums = lax.fori_loop(0, NP // QB, inner, (zero,) * (2 * PB if both else PB))
            for j in range(PB):
                even_part[k, b * PB + j] = sums[j]
                if both:
                    odd_part[o, b * PB + j] = sums[PB + j]
            return 0

        lax.fori_loop(0, NP // PB, block, 0)

    def interface(k, low_at, top_at, which):
        ratio = jnp.zeros((8, 128), F32)
        reduced = jnp.zeros((8, 128), F32)
        ratios, reduceds = [], []
        for s in range(NS - 1):
            lower = row(slopes, k, s, 2, slice(2, 3), slice(None))
            middle = row(slopes, k, s, 2, slice(3, 4), slice(None)) - row(slopes, k, s + 1, 2, slice(0, 1), slice(None))
            upper = -row(slopes, k, s + 1, 2, slice(1, 2), slice(None))
            right = slopes[k, s + 1, low_at] - slopes[k, s, top_at]
            pivot = middle - lower * ratio
            ratio = upper / pivot
            reduced = (right - lower * reduced) / pivot
            ratios.append(ratio)
            reduceds.append(reduced)
        later = jnp.zeros((8, 128), F32)
        values[which, 0] = later
        values[which, NS] = later
        for s in range(NS - 2, -1, -1):
            later = reduceds[s] - ratios[s] * later
            values[which, s + 1] = later
        return values[which, sub], values[which, sub + 1]

    def finish_step(k):
        f, t = STEPS[k]
        o = odd_index(k)
        for copy in slope_copies(k):
            copy.wait()
        below, above = interface(k, 0, 1, 0)
        if has_odd(k):
            odd_below, odd_above = interface(k, 3, 4, 1)
        position = lane + t * 128
        even_kept = position >= even_mode
        meets = position == even_mode
        merged = f * 2 + 1 - t

        def block(b, _):
            last = jnp.zeros((8, 128), F32)
            for i in range(4):
                p = b * 4 + i
                first = row(inv, k, p, slice(0, 1), slice(None))
                final = row(inv, k, p, slice(NP - 1, NP), slice(None))
                field = even_part[k, p] + below * first
                field = field + above * final
                if has_odd(k):
                    other = odd_part[o, p] + odd_below * first
                    other = other + odd_above * final
                    odd_flip[o, p] = flip_lanes(other)
                else:
                    other = odd_flip[merged, p]
                    at = f * 32 + i * 8
                    value = jnp.sum(jnp.where(meets, other, 0.0), axis=1, keepdims=True)
                    last = last + jnp.where(lane == iota(0) + at, value, 0.0)
                    field = jnp.where(even_kept, field, other)
                sent[k, p] = field
            if not has_odd(k):
                if k == 1:
                    lasts[b] = last
                else:
                    lasts[b] = lasts[b] + last
            return 0

        lax.fori_loop(0, NM, block, 0)
        packed[k, me] = sent[k, pl.ds(me * 4, 4)]

    def field_copies(k):
        return [
            pltpu.make_async_remote_copy(
                sent.at[k, pl.ds(other * 4, 4)], packed.at[k, me], field_send.at[k, i], field_recv.at[k, i],
                device_id={"ma": other}, device_id_type=MESH,
            )
            for i, other in enumerate(peers)
        ]

    def mode_copies():
        return [
            pltpu.make_async_remote_copy(
                own_modes, modes.at[me], mode_send.at[i], mode_recv.at[i],
                device_id={"ma": other}, device_id_type=MESH,
            )
            for i, other in enumerate(peers)
        ]

    def last_copies():
        return [
            pltpu.make_async_remote_copy(
                last_rows.at[other], extras.at[me], last_send.at[i], last_recv.at[i],
                device_id={"ma": other}, device_id_type=MESH,
            )
            for i, other in enumerate(peers)
        ]

    def start(copies):
        for copy in copies:
            copy.start()

    slope_step(0)
    pl.semaphore_wait(barrier, len(subs) + len(peers))
    start(slope_copies(0))
    start(mode_copies())
    particular_step(0)
    slope_step(1)
    start(slope_copies(1))
    particular_step(1)
    slope_step(2)
    start(slope_copies(2))
    for k in range(NSTEP):
        finish_step(k)
        start(field_copies(k))
        if k + 2 < NSTEP:
            particular_step(k + 2)
        if k + 3 < NSTEP:
            slope_step(k + 3)
            start(slope_copies(k + 3))

    for a in range(NM):
        last_rows[a] = jnp.sum(lasts[a], axis=0, keepdims=True)
    start(last_copies())
    extras[me] = last_rows[me]
    modes[me] = own_modes[...]
    for copies in [mode_copies()] + [field_copies(k) for k in range(NSTEP)] + [last_copies()]:
        for copy in copies:
            copy.wait()


def unpack_kernel(packed, extras, modes, out):
    step = pl.program_id(0)
    f = step // 4
    p = lax.rem(step, 4)
    lane = iota(1)
    sublane = iota(0)
    is_odd = lax.rem(sublane, 2) == 1
    at = {t: TILES.index(t) for t in TILES}
    pick = [sublane // 2, sublane // 2 + 4]

    def spread(value, c):
        return jnp.take_along_axis(value, pick[c], axis=0)

    def block(a, _):
        mode = modes[a].astype(jnp.int32)
        chosen = jnp.where(lane == f * 32 + p * 8 + sublane, jnp.broadcast_to(extras[a], (8, 128)), 0.0)
        extra = jnp.broadcast_to(jnp.sum(chosen, axis=1, keepdims=True), (8, 128))
        for t in range(4):
            value = packed[f * 4 + at[t], a, p]
            rows = pl.ds(pl.multiple_of(a * 8, 8), 8)
            if t < 2:
                even = jnp.where(lane + t * 128 >= mode, value, 0.0)
                other = None
            else:
                even = value
                merged = packed[f * 4 + at[3 - t], a, p]
                position = lane + (3 - t) * 128
                other = jnp.where(position < mode, merged, jnp.where(position == mode, extra, 0.0))
                other = flip_lanes(other)
            for c in range(2):
                tile = jnp.where(is_odd, 0.0 if other is None else spread(other, c), spread(even, c))
                out[0, 0, c, rows, t * 128 : t * 128 + 128] = tile
        return 0

    lax.fori_loop(0, NM, block, 0)


def body(forcing, slot_wavenumber, inverse, edge_weights):
    vmem = pl.BlockSpec(memory_space=pltpu.VMEM)
    smem = pl.BlockSpec(memory_space=pltpu.SMEM)
    anywhere = pl.BlockSpec(memory_space=pl.ANY)
    dma = pltpu.SemaphoreType.DMA
    packed, extras, modes = pl.pallas_call(
        solve_kernel,
        out_shape=(
            jax.ShapeDtypeStruct((NSTEP, NM, 4, 8, 128), F32),
            jax.ShapeDtypeStruct((NM, 1, 128), F32),
            jax.ShapeDtypeStruct((NM, 8, 128), F32),
        ),
        in_specs=[anywhere, smem, smem, anywhere],
        out_specs=(vmem, vmem, vmem),
        scratch_shapes=[
            pltpu.VMEM((NSTEP, NP, NP, 128), F32),
            pltpu.VMEM((NSTEP, NP, 16, 128), F32),
            pltpu.VMEM((NSTEP, NP, 8, 128), F32),
            pltpu.VMEM((4, NP, 8, 128), F32),
            pltpu.VMEM((NSTEP, NP, 8, 128), F32),
            pltpu.VMEM((4, NP, 8, 128), F32),
            pltpu.VMEM((4, NP, 8, 128), F32),
            pltpu.VMEM((NSTEP, NP, 8, 128), F32),
            pltpu.VMEM((2, NP, 128), F32),
            pltpu.VMEM((NSTEP, NS, 5, 8, 128), F32),
            pltpu.VMEM((2, NS + 1, 8, 128), F32),
            pltpu.VMEM((NM, 8, 128), F32),
            pltpu.VMEM((NM, 1, 128), F32),
            pltpu.VMEM((8, 128), F32),
            dma((NSTEP,)),
            dma((NSTEP,)),
            dma((NSTEP, NS - 1)),
            dma((NSTEP, NS - 1)),
            dma((NSTEP, NM - 1)),
            dma((NSTEP, NM - 1)),
            dma((NM - 1,)),
            dma((NM - 1,)),
            dma((NM - 1,)),
            dma((NM - 1,)),
        ],
        compiler_params=pltpu.CompilerParams(
            collective_id=0, has_side_effects=True, vmem_limit_bytes=48 * 1024 * 1024
        ),
        name="solve_and_exchange",
    )(forcing.reshape(2, NP, 16, 512), slot_wavenumber, edge_weights, inverse[0])
    return pl.pallas_call(
        unpack_kernel,
        out_shape=jax.ShapeDtypeStruct((2, 4, 2, 128, 512), F32),
        grid=(8,),
        in_specs=[vmem, vmem, vmem],
        out_specs=pl.BlockSpec((1, 1, 2, 128, 512), lambda i: (i // 4, lax.rem(i, 4), 0, 0, 0)),
        compiler_params=pltpu.CompilerParams(vmem_limit_bytes=16 * 1024 * 1024),
        name="unpack",
    )(packed, extras, modes)


def solution(mesh):
    return jax.shard_map(
        body,
        mesh=mesh,
        in_specs=(
            P(None, "sub", None, "ma", None),
            P("ma"),
            P("sub", None, None, None, None),
            P("sub", None, None),
        ),
        out_specs=P(None, ("sub", "ma"), None, None, None),
        check_vma=False,
    )
```

time: 235 us -> 74.6 us (0.32)
  Pallas kernels: 0 us -> 73.1 us
  matrix products: 70.3 us -> 0 us
  local copies, waits for them, and re-layouts: 68.2 us -> 1.33 us
  blocking collectives: 56.5 us -> 0 us
  waiting for transfers between devices: 15.9 us -> 0 us
  other arithmetic: 14.9 us -> 0 us
  starting transfers between devices: 6.8 us -> 0 us
    pallas_call x0 -> x2, Pallas kernels: none -> 73.1 us  [the longest x1 51.3 us: body(): pl.pallas_call(solve_kernel, out_shape=(jax.ShapeDtypeStruct((NSTEP, NM,...]
    dot_general x7 -> x0, matrix products: 70.3 us -> none  [the longest x1 57.6 us: body(): jnp.einsum('fpql,fqcml->fpcml', block_inverse, source, precision=HIGH)]
    all_to_all x1 -> x0, blocking collectives: 56.5 us -> none  [body(): lax.all_to_all(solution, 'ma', split_axis=1, concat_axis=3, tiled=True)]
    squeeze x1 -> x0, local copies, waits for them, and re-layouts: 30.5 us -> none  [body(): block_inverse = inverse[0]]
    all_to_all x1 -> x0, waiting for transfers between devices: 15.9 us -> none  [sent_to_all(): return lax.all_to_all(copies, axis, split_axis=0, concat_axis=0, tiled=True)]
    mul x11 -> x0, local copies, waits for them, and re-layouts: 9.8 us -> none  [the longest x1 8.66 us: body(): forcing * kept_modes[None, None, None, :, :]]
    add x1 -> x0, other arithmetic: 8.58 us -> none  [body(): solution = solution + upper_value[:, None] * upper_unit[:, :, None, None, :]]
    dot_general x7 -> x0, local copies, waits for them, and re-layouts: 7.74 us -> none  [the longest x2 7.68 us: body(): jnp.einsum('p,fpcml->fcml', edge_rows[1], particular, precision=HIGH)]
  transfers between devices with their start and end apart: 1 -> 0, of which waited for: 1 -> 0; matrix products, arithmetic and copies ran while one was open for 0% -> 0% of each run, Pallas kernels for 0% -> 0%
where the time goes in v1:
time: 74.6 us; the launch traced here: 74.4 us
  Pallas kernels  73.1 us (98%)
  local copies, waits for them, and re-layouts  1.33 us (2%)
    pallas_call x1, Pallas kernels, body(): pl.pallas_call(solve_kernel, out_shape=(jax.ShapeDtypeStruct((NSTEP, NM,...  51.3 us
    pallas_call x1, Pallas kernels, body(): pl.pallas_call(unpack_kernel, out_shape=jax.ShapeDtypeStruct((2, 4, 2, 12...  21.8 us

profile of v1, /device:TPU:1, one launch (start us, length us, event | category | flops | bytes accessed | tf_op | source)
XLA Modules:
  0.0 74.4 jit_solution(12003162386937304936)
XLA Ops:
  0.0 0.0 copy-start
  0.0 0.7 copy-done
  0.7 0.0 copy-start.1
  0.7 0.7 copy-done.1
  1.3 51.3 %solve_and_exchange.1 = (f32[8,16,4,8,128]{4,3,2,1,0:T(8,128)S(1)}, f32[16,1,128]{2,1,0:T(1,128)S(1)}, f32[16,8,128]{2,1,0:T(8,128)S(1)}) custom-call(f32[2,64,16,512]{3,2,1,0:T(8,128)} %bitcast.3, s32[8]{0:T(128)S(1)} %copy-done.1, f32[1,2,64]{2,1,0:T(2,128)S(1)} %copy-done, f32[2,64,64,512]{3,2,1,0:T(8,128)} %bitcast.2), custom_call_target="tpu_custom_call" | custom-call | tf_op jit(solution)/shard_map/solve_and_exchange/pallas_call | solution.py:350
  52.7 21.8 %unpack.1 = f32[2,4,2,128,512]{4,3,2,1,0:T(8,128)} custom-call(f32[8,16,4,8,128]{4,3,2,1,0:T(8,128)S(1)} %get-tuple-element.8.packed, f32[16,1,128]{2,1,0:T(1,128)S(1)} %get-tuple-element.9.extras, f32[16,8,128]{2,1,0:T(8,128)S(1)} %get-tuple-element.10.modes), custom_call_target="tpu_custom_call" | custom-call | tf_op jit(solution)/shard_map/unpack/pallas_call | solution.py:390
Async XLA Ops:
  0.0 0.7 copy-start
  0.7 0.7 copy-start.1

commit v2 on v0

v2 whole, which is shorter than its diff:
```python
import jax
import jax.numpy as jnp
from jax import lax
from jax.experimental import pallas as pl
from jax.experimental.pallas import tpu as pltpu
from jax.sharding import PartitionSpec as P

MESH = pl.DeviceIdType.MESH
F32 = jnp.float32
NP = 64
NS = 8
NM = 16
TILES = (2, 1, 3, 0)
STEPS = tuple((f, t) for f in range(2) for t in TILES)
NSTEP = len(STEPS)
AHEAD = 3
PB = 8
QB = 31
FB = 32
ORDER = "S0 S1 P0 S2 F0 P1 F1 S3 S4 P2 F2 S5 S6 P3 F3 S7 P4 F4 P5 F5 P6 F6 P7 F7"


def has_odd(k):
    return STEPS[k][1] >= 2


def half(k):
    return k // 2


def iota(dim):
    return lax.broadcasted_iota(jnp.int32, (8, 128), dim)


def row(ref, *at):
    return jnp.broadcast_to(ref[at], (8, 128))


def flip_lanes(x):
    return jnp.take_along_axis(x, 127 - iota(1), axis=1)


def solve_kernel(
    forcing, slot_hbm, edge_hbm, inverse, out,
    slots, edges, inv, raw, even, odd, even_part, odd_part, odd_flip, sent, packed, weights, splats,
    even_slopes, odd_slopes, factors, values, last_rows, extras, own_modes, modes,
    small_sem, inv_sem, raw_sem, even_send, even_recv, odd_send, odd_recv,
    field_send, field_recv, last_send, last_recv, mode_send, mode_recv,
):
    sub = lax.axis_index("sub")
    me = lax.axis_index("ma")
    y, x = me // 4, lax.rem(me, 4)
    subs = [lax.rem(sub + d, NS) for d in range(1, NS)]
    peers = []
    for dy in (2, 1, 3, 0):
        for dx in (2, 1, 3, 0):
            if dy or dx:
                peers.append(lax.rem(y + dy, 4) * 4 + lax.rem(x + dx, 4))

    def load(k):
        f, t = STEPS[k]
        lanes = pl.ds(t * 128, 128)
        return (
            pltpu.make_async_copy(inverse.at[f, :, :, lanes], inv.at[k], inv_sem.at[k]),
            pltpu.make_async_copy(forcing.at[f, :, :, lanes], raw.at[k], raw_sem.at[k]),
        )

    def start(copies):
        for copy in copies:
            copy.start()

    start(load(0))
    small = (
        pltpu.make_async_copy(slot_hbm, slots, small_sem.at[0]),
        pltpu.make_async_copy(edge_hbm, edges, small_sem.at[1]),
    )
    start(small)
    barrier = pltpu.get_barrier_semaphore()
    for other in subs:
        pl.semaphore_signal(barrier, inc=1, device_id={"sub": other}, device_id_type=MESH)
    for other in peers:
        pl.semaphore_signal(barrier, inc=1, device_id={"ma": other}, device_id_type=MESH)
    for k in range(1, AHEAD):
        start(load(k))

    for copy in small:
        copy.wait()
    zero = jnp.zeros((8, 128), F32)
    lane = iota(1)
    sublane = iota(0)
    pair = lax.rem(sublane, 4)
    even_mode = jnp.zeros((8, 128), jnp.int32)
    odd_mode = jnp.zeros((8, 128), jnp.int32)
    for j in range(4):
        even_mode = jnp.where(pair == j, slots[2 * j], even_mode)
        odd_mode = jnp.where(pair == j, slots[2 * j + 1], odd_mode)
    own_modes[...] = even_mode.astype(F32)
    for e in range(2):
        for p in range(NP):
            splats[e, p] = jnp.full((8, 128), edges[0, e, p], F32)

    def prepare(k, which):
        f, t = STEPS[k]
        kept = lane + t * 128 >= (even_mode if which == 0 else odd_mode)
        target = even.at[k] if which == 0 else odd.at[half(k)]

        def block(b, _):
            for i in range(8):
                q = b * 8 + i
                target[q] = jnp.where(kept, raw[k, q, pl.ds(which, 8, stride=2), :], zero)
            return 0

        lax.fori_loop(0, NP // 8, block, 0)
        target[0] = zero
        target[NP - 1] = zero

    def weigh(k):
        def block(b, _):
            def inner(c, sums):
                sums = list(sums)
                for j in range(16):
                    p = c * 16 + j
                    low, top = splats[0, p], splats[1, p]
                    for i in range(4):
                        tile = inv[k, p, pl.ds(pl.multiple_of(b * 32 + i * 8, 8), 8), :]
                        sums[i] = sums[i] + low * tile
                        sums[4 + i] = sums[4 + i] + top * tile
                return tuple(sums)

            sums = lax.fori_loop(0, NP // 16, inner, (zero,) * 8)
            for i in range(4):
                rows = pl.ds(pl.multiple_of(b * 32 + i * 8, 8), 8)
                weights[0, rows, :] = sums[i]
                weights[1, rows, :] = sums[4 + i]
            return 0

        lax.fori_loop(0, NP // 32, block, 0)

    def slope_sums(k, which):
        source = even.at[k] if which == 0 else odd.at[half(k)]
        def block(b, sums):
            sums = list(sums)
            for i in range(8):
                q = b * 8 + i
                for e in range(2):
                    at = 2 * e + i % 2
                    sums[at] = sums[at] + row(weights, e, pl.ds(q, 1), slice(None)) * source[q]
            return tuple(sums)

        sums = lax.fori_loop(0, NP // 8, block, (zero,) * 4)
        return sums[0] + sums[1], sums[2] + sums[3]

    def even_copies(k):
        here = even_slopes.at[k, sub]
        return [
            pltpu.make_async_remote_copy(
                here, here, even_send.at[k], even_recv.at[k], device_id={"sub": other}, device_id_type=MESH
            )
            for other in subs
        ]

    def odd_copies(k):
        here = odd_slopes.at[half(k), sub]
        return [
            pltpu.make_async_remote_copy(
                here, here, odd_send.at[half(k)], odd_recv.at[half(k)], device_id={"sub": other}, device_id_type=MESH
            )
            for other in subs
        ]

    def even_all(k):
        most = even_slopes.at[k, pl.ds(0, NS - 1)]
        return pltpu.make_async_remote_copy(
            most, most, even_send.at[k], even_recv.at[k], device_id={"sub": subs[0]}, device_id_type=MESH
        )

    def odd_all(k):
        most = odd_slopes.at[half(k), pl.ds(0, NS - 1)]
        return pltpu.make_async_remote_copy(
            most, most, odd_send.at[half(k)], odd_recv.at[half(k)], device_id={"sub": subs[0]}, device_id_type=MESH
        )

    def slope_step(k, before_send=None):
        for copy in load(k):
            copy.wait()
        if k + AHEAD < NSTEP:
            start(load(k + AHEAD))
        prepare(k, 0)
        weigh(k)
        low, top = slope_sums(k, 0)
        even_slopes[k, sub, 0] = low
        even_slopes[k, sub, 1] = top
        for e in range(2):
            for i, q in enumerate((0, NP - 1)):
                even_slopes[k, sub, 2, 2 * e + i : 2 * e + i + 1, :] = weights[e, q : q + 1, :]
        if before_send is not None:
            before_send()
        start(even_copies(k))
        if has_odd(k):
            prepare(k, 1)
            low, top = slope_sums(k, 1)
            odd_slopes[half(k), sub, 0] = low
            odd_slopes[half(k), sub, 1] = top
            start(odd_copies(k))

    def ends(k, p):
        return (
            row(inv, k, p, slice(0, 1), slice(None)),
            row(inv, k, p, slice(NP - 1, NP), slice(None)),
        )

    def particular_step(k):
        both = has_odd(k)
        o = half(k)

        def block(b, _):
            def inner(c, sums):
                sums = list(sums)
                for i in range(QB):
                    q = 1 + c * QB + i
                    source = even[k, q]
                    other = odd[o, q] if both else None
                    for j in range(PB):
                        weight = row(inv, k, b * PB + j, pl.ds(q, 1), slice(None))
                        sums[j] = sums[j] + weight * source
                        if both:
                            sums[PB + j] = sums[PB + j] + weight * other
                return tuple(sums)

            sums = lax.fori_loop(0, (NP - 2) // QB, inner, (zero,) * (2 * PB if both else PB))
            for j in range(PB):
                p = b * PB + j
                even_part[k, p] = sums[j]
                if both:
                    odd_part[o, p] = sums[PB + j]
            return 0

        lax.fori_loop(0, NP // PB, block, 0)

    def factor(k):
        def influence(s, i):
            return row(even_slopes, k, s, 2, slice(i, i + 1), slice(None))

        last = NS - 2
        lower = [influence(s, 2) for s in range(NS - 1)]
        middle = [influence(s, 3) - influence(s + 1, 0) for s in range(NS - 1)]
        upper = [-influence(s + 1, 1) for s in range(NS - 1)]
        ratio = [zero] * (NS - 1)
        scale = [zero] * (NS - 1)
        for s in range(3):
            scale[s] = 1.0 / (middle[s] - lower[s] * ratio[s - 1] if s else middle[s])
            ratio[s] = upper[s] * scale[s]
            r = last - s
            scale[r] = 1.0 / (middle[r] - upper[r] * ratio[r + 1] if s else middle[r])
            ratio[r] = lower[r] * scale[r]
        scale[3] = 1.0 / ((middle[3] - lower[3] * ratio[2]) - upper[3] * ratio[4])
        for s in range(NS - 1):
            factors[0, s] = lower[s]
            factors[1, s] = upper[s]
            factors[2, s] = ratio[s]
            factors[3, s] = scale[s]

    def interface(k, which):
        slopes = even_slopes.at[k] if which == 0 else odd_slopes.at[half(k)]
        last = NS - 2
        right = [slopes[s + 1, 0] - slopes[s, 1] for s in range(NS - 1)]
        lower = [factors[0, s] for s in range(NS - 1)]
        upper = [factors[1, s] for s in range(NS - 1)]
        ratio = [factors[2, s] for s in range(NS - 1)]
        scale = [factors[3, s] for s in range(NS - 1)]
        reduced = [zero] * (NS - 1)
        for s in range(3):
            r = last - s
            reduced[s] = (right[s] - lower[s] * reduced[s - 1] if s else right[s]) * scale[s]
            reduced[r] = (right[r] - upper[r] * reduced[r + 1] if s else right[r]) * scale[r]
        found = [zero] * (NS - 1)
        found[3] = ((right[3] - lower[3] * reduced[2]) - upper[3] * reduced[4]) * scale[3]
        for s in (2, 1, 0):
            found[s] = reduced[s] - ratio[s] * found[s + 1]
            found[last - s] = reduced[last - s] - ratio[last - s] * found[last - s - 1]
        values[which, 0] = zero
        values[which, NS] = zero
        for s in range(NS - 1):
            values[which, s + 1] = found[s]
        return values[which, sub], values[which, sub + 1]

    def finish_step(k):
        f, t = STEPS[k]
        u = half(k)
        even_all(k).wait()
        factor(k)
        below, above = interface(k, 0)
        position = lane + t * 128
        even_kept = position >= even_mode

        def block(b, _):
            for i in range(FB):
                p = b * FB + i
                first, final = ends(k, p)
                field = (even_part[k, p] + below * first) + above * final
                if not has_odd(k):
                    field = jnp.where(even_kept, field, odd_flip[u, p])
                sent[k, p] = field
            return 0

        lax.fori_loop(0, NP // FB, block, 0)
        packed[k, me] = sent[k, pl.ds(me * 4, 4)]
        start(field_copies(k))
        if has_odd(k):
            odd_all(k).wait()
            odd_below, odd_above = interface(k, 1)
            meets = lane + (3 - t) * 128 == even_mode

            def odd_block(b, _):
                for a in range(FB // 4):
                    last = zero
                    for i in range(4):
                        p = b * FB + a * 4 + i
                        first, final = ends(k, p)
                        other = flip_lanes((odd_part[u, p] + odd_below * first) + odd_above * final)
                        odd_flip[u, p] = other
                        value = jnp.sum(jnp.where(meets, other, 0.0), axis=1, keepdims=True)
                        last = jnp.where(lane == sublane + i * 8, value, last)
                    last_rows[u, b * (FB // 4) + a] = jnp.sum(last, axis=0, keepdims=True)
                return 0

            lax.fori_loop(0, NP // FB, odd_block, 0)
            extras[u, me] = last_rows[u, me]
            start(last_copies(u))

    def field_copies(k):
        return [
            pltpu.make_async_remote_copy(
                sent.at[k, pl.ds(other * 4, 4)], packed.at[k, me], field_send.at[k], field_recv.at[k],
                device_id={"ma": other}, device_id_type=MESH,
            )
            for other in peers
        ]

    def field_all(k):
        return pltpu.make_async_remote_copy(
            sent.at[k, pl.ds(0, NP - 4)], packed.at[k, pl.ds(0, NM - 1)], field_send.at[k], field_recv.at[k],
            device_id={"ma": peers[0]}, device_id_type=MESH,
        )

    def last_copies(u):
        return [
            pltpu.make_async_remote_copy(
                last_rows.at[u, other], extras.at[u, me], last_send.at[u], last_recv.at[u],
                device_id={"ma": other}, device_id_type=MESH,
            )
            for other in peers
        ]

    def last_all(u):
        return pltpu.make_async_remote_copy(
            last_rows.at[u, pl.ds(0, NM - 1)], extras.at[u, pl.ds(0, NM - 1)], last_send.at[u], last_recv.at[u],
            device_id={"ma": peers[0]}, device_id_type=MESH,
        )

    def mode_copies():
        return [
            pltpu.make_async_remote_copy(
                own_modes, modes.at[me], mode_send, mode_recv, device_id={"ma": other}, device_id_type=MESH
            )
            for other in peers
        ]

    def mode_all():
        most = modes.at[pl.ds(0, NM - 1)]
        return pltpu.make_async_remote_copy(
            most, most, mode_send, mode_recv, device_id={"ma": peers[0]}, device_id_type=MESH
        )

    def unpack(u):
        f, t = STEPS[2 * u]
        near = 3 - t
        is_odd = lax.rem(sublane, 2) == 1
        pick = [sublane // 2, sublane // 2 + 4]

        def spread(value, c):
            return jnp.take_along_axis(value, pick[c], axis=0)

        def block(b, _):
            for i in range(4):
                a = b * 4 + i
                mode = modes[a].astype(jnp.int32)
                even_kept = lane + near * 128 >= mode
                odd_at = lane + t * 128 + mode
                rows = pl.ds(pl.multiple_of(a * 8, 8), 8)
                row_extras = row(extras, u, a)
                for p in range(4):
                    merged = packed[2 * u + 1, a, p]
                    extra = jnp.take_along_axis(row_extras, sublane + p * 8, axis=1)
                    other = jnp.where(odd_at > 511, flip_lanes(merged), jnp.where(odd_at == 511, extra, 0.0))
                    far = packed[2 * u, a, p]
                    close = jnp.where(even_kept, merged, 0.0)
                    for c in range(2):
                        out[f, p, c, rows, t * 128 : t * 128 + 128] = jnp.where(
                            is_odd, spread(other, c), spread(far, c)
                        )
                        out[f, p, c, rows, near * 128 : near * 128 + 128] = jnp.where(is_odd, 0.0, spread(close, c))
            return 0

        lax.fori_loop(0, NM // 4, block, 0)

    def greet():
        pl.semaphore_wait(barrier, len(subs) + len(peers))
        modes[me] = own_modes[...]

    for item in ORDER.split():
        k = int(item[1])
        if item[0] == "S":
            slope_step(k, greet if k == 0 else None)
            if k == 0:
                start(mode_copies())
        elif item[0] == "P":
            particular_step(k)
        else:
            finish_step(k)

    mode_all().wait()
    for u in range(NSTEP // 2):
        field_all(2 * u).wait()
        field_all(2 * u + 1).wait()
        last_all(u).wait()
        unpack(u)


def body(forcing, slot_wavenumber, inverse, edge_weights):
    vmem = pl.BlockSpec(memory_space=pltpu.VMEM)
    anywhere = pl.BlockSpec(memory_space=pl.ANY)
    dma = pltpu.SemaphoreType.DMA
    units = NSTEP // 2
    return pl.pallas_call(
        solve_kernel,
        out_shape=jax.ShapeDtypeStruct((2, 4, 2, 128, 512), F32),
        in_specs=[anywhere] * 4,
        out_specs=vmem,
        scratch_shapes=[
            pltpu.SMEM((8,), jnp.int32),
            pltpu.SMEM((1, 2, NP), F32),
            pltpu.VMEM((NSTEP, NP, NP, 128), F32),
            pltpu.VMEM((NSTEP, NP, 16, 128), F32),
            pltpu.VMEM((NSTEP, NP, 8, 128), F32),
            pltpu.VMEM((units, NP, 8, 128), F32),
            pltpu.VMEM((NSTEP, NP, 8, 128), F32),
            pltpu.VMEM((units, NP, 8, 128), F32),
            pltpu.VMEM((units, NP, 8, 128), F32),
            pltpu.VMEM((NSTEP, NP, 8, 128), F32),
            pltpu.VMEM((NSTEP, NM, 4, 8, 128), F32),
            pltpu.VMEM((2, NP, 128), F32),
            pltpu.VMEM((2, NP, 8, 128), F32),
            pltpu.VMEM((NSTEP, NS, 3, 8, 128), F32),
            pltpu.VMEM((units, NS, 2, 8, 128), F32),
            pltpu.VMEM((4, NS - 1, 8, 128), F32),
            pltpu.VMEM((2, NS + 1, 8, 128), F32),
            pltpu.VMEM((units, NM, 1, 128), F32),
            pltpu.VMEM((units, NM, 1, 128), F32),
            pltpu.VMEM((8, 128), F32),
            pltpu.VMEM((NM, 8, 128), F32),
            dma((2,)),
            dma((NSTEP,)),
            dma((NSTEP,)),
            dma((NSTEP,)),
            dma((NSTEP,)),
            dma((units,)),
            dma((units,)),
            dma((NSTEP,)),
            dma((NSTEP,)),
            dma((units,)),
            dma((units,)),
            dma,
            dma,
        ],
        compiler_params=pltpu.CompilerParams(
            collective_id=0, has_side_effects=True, vmem_limit_bytes=48 * 1024 * 1024
        ),
        name="solve_and_exchange",
    )(forcing.reshape(2, NP, 16, 512), slot_wavenumber, edge_weights, inverse[0])


def solution(mesh):
    return jax.shard_map(
        body,
        mesh=mesh,
        in_specs=(
            P(None, "sub", None, "ma", None),
            P("ma"),
            P("sub", None, None, None, None),
            P("sub", None, None),
        ),
        out_specs=P(None, ("sub", "ma"), None, None, None),
        check_vma=False,
    )
```

time: 235 us -> 43.6 us (0.19)
  matrix products: 70.3 us -> 0 us
  local copies, waits for them, and re-layouts: 68.2 us -> 3.35 us
  blocking collectives: 56.5 us -> 0 us
  Pallas kernels: 0 us -> 40.1 us
  waiting for transfers between devices: 15.9 us -> 0 us
  other arithmetic: 14.9 us -> 0 us
  starting transfers between devices: 6.8 us -> 0 us
    dot_general x7 -> x0, matrix products: 70.3 us -> none  [the longest x1 57.6 us: body(): jnp.einsum('fpql,fqcml->fpcml', block_inverse, source, precision=HIGH)]
    all_to_all x1 -> x0, blocking collectives: 56.5 us -> none  [body(): lax.all_to_all(solution, 'ma', split_axis=1, concat_axis=3, tiled=True)]
    pallas_call x0 -> x1, Pallas kernels: none -> 40.1 us  [body(): pl.pallas_call(solve_kernel, out_shape=jax.ShapeDtypeStruct((2, 4, 2, 128...]
    squeeze x1 -> x0, local copies, waits for them, and re-layouts: 30.5 us -> none  [body(): block_inverse = inverse[0]]
    all_to_all x1 -> x0, waiting for transfers between devices: 15.9 us -> none  [sent_to_all(): return lax.all_to_all(copies, axis, split_axis=0, concat_axis=0, tiled=True)]
    mul x11 -> x0, local copies, waits for them, and re-layouts: 9.8 us -> none  [the longest x1 8.66 us: body(): forcing * kept_modes[None, None, None, :, :]]
    add x1 -> x0, other arithmetic: 8.58 us -> none  [body(): solution = solution + upper_value[:, None] * upper_unit[:, :, None, None, :]]
    dot_general x7 -> x0, local copies, waits for them, and re-layouts: 7.74 us -> none  [the longest x2 7.68 us: body(): jnp.einsum('p,fpcml->fcml', edge_rows[1], particular, precision=HIGH)]
  transfers between devices with their start and end apart: 1 -> 0, of which waited for: 1 -> 0; matrix products, arithmetic and copies ran while one was open for 0% -> 0% of each run, Pallas kernels for 0% -> 0%
where the time goes in v2:
time: 43.6 us; the launch traced here: 43.4 us
  Pallas kernels  40.1 us (92%)
  local copies, waits for them, and re-layouts  3.35 us (8%)
    pallas_call x1, Pallas kernels, body(): pl.pallas_call(solve_kernel, out_shape=jax.ShapeDtypeStruct((2, 4, 2, 128...  40.1 us
    unnamed x5, local copies, waits for them, and re-layouts  3.35 us

profile of v2, /device:TPU:1, one launch (start us, length us, event | category | flops | bytes accessed | tf_op | source)
XLA Modules:
  0.0 43.4 jit_solution(2207906198999935456)
XLA Ops:
  0.0 0.0 copy-start
  0.0 0.7 %copy-done = f32[1,2,64]{2,1,0:T(2,128)S(1)} copy-done((f32[1,2,64]{2,1,0:T(2,128)S(1)}, f32[1,2,64]{2,1,0:T(2,128)}, u32[]{:S(2)}) %copy-start) | copy-done | bytes 536
  0.7 0.0 copy-start.1
  0.7 0.7 %copy-done.1 = s32[8]{0:T(128)S(1)} copy-done((s32[8]{0:T(128)S(1)}, s32[8]{0:T(128)}, u32[]{:S(2)}) %copy-start.1) | copy-done | bytes 56
  1.3 40.1 %solve_and_exchange.1 = f32[2,4,2,128,512]{4,3,2,1,0:T(8,128)S(1)} custom-call(f32[2,64,16,512]{3,2,1,0:T(8,128)} %bitcast.3, s32[8]{0:T(128)S(1)} %copy-done.1, f32[1,2,64]{2,1,0:T(2,128)S(1)} %copy-done, f32[2,64,64,512]{3,2,1,0:T(8,128)} %bitcast.2), custom_call_target="tpu_custom_call" | custom-call | tf_op jit(solution)/shard_map/solve_and_exchange/pallas_call | solution.py:435
  41.4 2.0 %copy.6 = f32[2,4,2,128,512]{4,3,2,1,0:T(8,128)} copy(f32[2,4,2,128,512]{4,3,2,1,0:T(8,128)S(1)} %solve_and_exchange.1) | data formatting | bytes 8388608
Async XLA Ops:
  0.0 0.7 %copy-start = (f32[1,2,64]{2,1,0:T(2,128)S(1)}, f32[1,2,64]{2,1,0:T(2,128)}, u32[]{:S(2)}) copy-start(f32[1,2,64]{2,1,0:T(2,128)} %edge_hbm.1) | copy-start | bytes 1540
  0.7 0.7 %copy-start.1 = (s32[8]{0:T(128)S(1)}, s32[8]{0:T(128)}, u32[]{:S(2)}) copy-start(s32[8]{0:T(128)} %slot_hbm.1) | copy-start | bytes 100

commit v3 on v2

--- a/solution.py
+++ b/solution.py
@@ -17,7 +17,7 @@
 PB = 8
 QB = 31
 FB = 32
-ORDER = "S0 S1 P0 S2 F0 P1 F1 S3 S4 P2 F2 S5 S6 P3 F3 S7 P4 F4 P5 F5 P6 F6 P7 F7"
+ORDER = ("S0", "E0", "R0", "S1", "O0", "S2", "P1", "F0", "F1", "S3", "P2", "F2", "S4", "P3", "F3", "S5", "P4", "F4", "S6", "P5", "F5", "S7", "P6", "F6", "P7", "F7")
 
 
 def has_odd(k):
@@ -43,14 +43,19 @@
 def solve_kernel(
     forcing, slot_hbm, edge_hbm, inverse, out,
     slots, edges, inv, raw, even, odd, even_part, odd_part, odd_flip, sent, packed, weights, splats,
-    even_slopes, odd_slopes, factors, values, last_rows, extras, own_modes, modes,
+    even_slopes, odd_slopes, factors, values, last_rows, extras, own_modes, modes, own_ends, far_ends,
     small_sem, inv_sem, raw_sem, even_send, even_recv, odd_send, odd_recv,
-    field_send, field_recv, last_send, last_recv, mode_send, mode_recv,
+    field_send, field_recv, last_send, last_recv, mode_send, mode_recv, end_send, end_recv,
 ):
     sub = lax.axis_index("sub")
     me = lax.axis_index("ma")
     y, x = me // 4, lax.rem(me, 4)
-    subs = [lax.rem(sub + d, NS) for d in range(1, NS)]
+    chip, core = sub // 2, lax.rem(sub, 2)
+    subs = []
+    for dz in (2, 1, 3, 0):
+        for dc in (0, 1):
+            if dz or dc:
+                subs.append(lax.rem(chip + dz, 4) * 2 + lax.rem(core + dc, 2))
     peers = []
     for dy in (2, 1, 3, 0):
         for dx in (2, 1, 3, 0):
@@ -61,8 +66,8 @@
         f, t = STEPS[k]
         lanes = pl.ds(t * 128, 128)
         return (
+            pltpu.make_async_copy(forcing.at[f, :, :, lanes], raw.at[k], raw_sem.at[k]),
             pltpu.make_async_copy(inverse.at[f, :, :, lanes], inv.at[k], inv_sem.at[k]),
-            pltpu.make_async_copy(forcing.at[f, :, :, lanes], raw.at[k], raw_sem.at[k]),
         )
 
     def start(copies):
@@ -181,11 +186,14 @@
         )
 
     def slope_step(k, before_send=None):
-        for copy in load(k):
-            copy.wait()
+        source_copy, inverse_copy = load(k)
+        source_copy.wait()
+        prepare(k, 0)
+        if has_odd(k):
+            prepare(k, 1)
+        inverse_copy.wait()
         if k + AHEAD < NSTEP:
             start(load(k + AHEAD))
-        prepare(k, 0)
         weigh(k)
         low, top = slope_sums(k, 0)
         even_slopes[k, sub, 0] = low
@@ -197,7 +205,6 @@
             before_send()
         start(even_copies(k))
         if has_odd(k):
-            prepare(k, 1)
             low, top = slope_sums(k, 1)
             odd_slopes[half(k), sub, 0] = low
             odd_slopes[half(k), sub, 1] = top
@@ -209,8 +216,7 @@
             row(inv, k, p, slice(NP - 1, NP), slice(None)),
         )
 
-    def particular_step(k):
-        both = has_odd(k)
+    def particular_step(k, parts):
         o = half(k)
 
         def block(b, _):
@@ -218,21 +224,21 @@
                 sums = list(sums)
                 for i in range(QB):
                     q = 1 + c * QB + i
-                    source = even[k, q]
-                    other = odd[o, q] if both else None
+                    sources = [even[k, q] if which == 0 else odd[o, q] for which in parts]
                     for j in range(PB):
                         weight = row(inv, k, b * PB + j, pl.ds(q, 1), slice(None))
-                        sums[j] = sums[j] + weight * source
-                        if both:
-                            sums[PB + j] = sums[PB + j] + weight * other
+                        for n, source in enumerate(sources):
+                            sums[n * PB + j] = sums[n * PB + j] + weight * source
                 return tuple(sums)
 
-            sums = lax.fori_loop(0, (NP - 2) // QB, inner, (zero,) * (2 * PB if both else PB))
+            sums = lax.fori_loop(0, (NP - 2) // QB, inner, (zero,) * (len(parts) * PB))
             for j in range(PB):
                 p = b * PB + j
-                even_part[k, p] = sums[j]
-                if both:
-                    odd_part[o, p] = sums[PB + j]
+                for n, which in enumerate(parts):
+                    if which == 0:
+                        even_part[k, p] = sums[n * PB + j]
+                    else:
+                        odd_part[o, p] = sums[n * PB + j]
             return 0
 
         lax.fori_loop(0, NP // PB, block, 0)
@@ -285,11 +291,23 @@
         return values[which, sub], values[which, sub + 1]
 
     def finish_step(k):
-        f, t = STEPS[k]
-        u = half(k)
         even_all(k).wait()
         factor(k)
         below, above = interface(k, 0)
+        if k == 0:
+            own_ends[0] = below
+            own_ends[1] = above
+            start(end_copies())
+            far_ends[me, 0] = below
+            far_ends[me, 1] = above
+        else:
+            correct_even(k, below, above)
+        if has_odd(k):
+            correct_odd(k)
+
+    def correct_even(k, below, above):
+        t = STEPS[k][1]
+        u = half(k)
         position = lane + t * 128
         even_kept = position >= even_mode
 
@@ -306,32 +324,52 @@
         lax.fori_loop(0, NP // FB, block, 0)
         packed[k, me] = sent[k, pl.ds(me * 4, 4)]
         start(field_copies(k))
-        if has_odd(k):
-            odd_all(k).wait()
-            odd_below, odd_above = interface(k, 1)
-            meets = lane + (3 - t) * 128 == even_mode
-
-            def odd_block(b, _):
-                for a in range(FB // 4):
-                    last = zero
-                    for i in range(4):
-                        p = b * FB + a * 4 + i
-                        first, final = ends(k, p)
-                        other = flip_lanes((odd_part[u, p] + odd_below * first) + odd_above * final)
-                        odd_flip[u, p] = other
-                        value = jnp.sum(jnp.where(meets, other, 0.0), axis=1, keepdims=True)
-                        last = jnp.where(lane == sublane + i * 8, value, last)
-                    last_rows[u, b * (FB // 4) + a] = jnp.sum(last, axis=0, keepdims=True)
-                return 0
-
-            lax.fori_loop(0, NP // FB, odd_block, 0)
-            extras[u, me] = last_rows[u, me]
-            start(last_copies(u))
+
+    def correct_odd(k):
+        t = STEPS[k][1]
+        u = half(k)
+        odd_all(k).wait()
+        below, above = interface(k, 1)
+        meets = lane + (3 - t) * 128 == even_mode
+
+        def block(b, _):
+            for a in range(FB // 4):
+                last = zero
+                for i in range(4):
+                    p = b * FB + a * 4 + i
+                    first, final = ends(k, p)
+                    other = flip_lanes((odd_part[u, p] + below * first) + above * final)
+                    odd_flip[u, p] = other
+                    value = jnp.sum(jnp.where(meets, other, 0.0), axis=1, keepdims=True)
+                    last = jnp.where(lane == sublane + i * 8, value, last)
+                last_rows[u, b * (FB // 4) + a] = jnp.sum(last, axis=0, keepdims=True)
+            return 0
+
+        lax.fori_loop(0, NP // FB, block, 0)
+        extras[u, me] = last_rows[u, me]
+        start(last_copies(u))
+
+    def field_source(k):
+        return even_part.at[k] if k == 0 else sent.at[k]
+
+    def end_copies():
+        return [
+            pltpu.make_async_remote_copy(
+                own_ends, far_ends.at[me], end_send, end_recv, device_id={"ma": other}, device_id_type=MESH
+            )
+            for other in peers
+        ]
+
+    def end_all():
+        most = far_ends.at[pl.ds(0, NM - 1)]
+        return pltpu.make_async_remote_copy(
+            most, most, end_send, end_recv, device_id={"ma": peers[0]}, device_id_type=MESH
+        )
 
     def field_copies(k):
         return [
             pltpu.make_async_remote_copy(
-                sent.at[k, pl.ds(other * 4, 4)], packed.at[k, me], field_send.at[k], field_recv.at[k],
+                field_source(k).at[pl.ds(other * 4, 4)], packed.at[k, me], field_send.at[k], field_recv.at[k],
                 device_id={"ma": other}, device_id_type=MESH,
             )
             for other in peers
@@ -339,7 +377,7 @@
 
     def field_all(k):
         return pltpu.make_async_remote_copy(
-            sent.at[k, pl.ds(0, NP - 4)], packed.at[k, pl.ds(0, NM - 1)], field_send.at[k], field_recv.at[k],
+            field_source(k).at[pl.ds(0, NP - 4)], packed.at[k, pl.ds(0, NM - 1)], field_send.at[k], field_recv.at[k],
             device_id={"ma": peers[0]}, device_id_type=MESH,
         )
 
@@ -378,12 +416,14 @@
         is_odd = lax.rem(sublane, 2) == 1
         pick = [sublane // 2, sublane // 2 + 4]
 
+        corrections = [ends(0, me * 4 + p) for p in range(4)] if u == 0 else None
+
         def spread(value, c):
             return jnp.take_along_axis(value, pick[c], axis=0)
 
         def block(b, _):
-            for i in range(4):
-                a = b * 4 + i
+            for i in range(8):
+                a = b * 8 + i
                 mode = modes[a].astype(jnp.int32)
                 even_kept = lane + near * 128 >= mode
                 odd_at = lane + t * 128 + mode
@@ -394,6 +434,8 @@
                     extra = jnp.take_along_axis(row_extras, sublane + p * 8, axis=1)
                     other = jnp.where(odd_at > 511, flip_lanes(merged), jnp.where(odd_at == 511, extra, 0.0))
                     far = packed[2 * u, a, p]
+                    if u == 0:
+                        far = (far + far_ends[a, 0] * corrections[p][0]) + far_ends[a, 1] * corrections[p][1]
                     close = jnp.where(even_kept, merged, 0.0)
                     for c in range(2):
                         out[f, p, c, rows, t * 128 : t * 128 + 128] = jnp.where(
@@ -402,24 +444,28 @@
                         out[f, p, c, rows, near * 128 : near * 128 + 128] = jnp.where(is_odd, 0.0, spread(close, c))
             return 0
 
-        lax.fori_loop(0, NM // 4, block, 0)
+        lax.fori_loop(0, NM // 8, block, 0)
 
     def greet():
         pl.semaphore_wait(barrier, len(subs) + len(peers))
         modes[me] = own_modes[...]
 
-    for item in ORDER.split():
+    for item in ORDER:
         k = int(item[1])
         if item[0] == "S":
             slope_step(k, greet if k == 0 else None)
             if k == 0:
                 start(mode_copies())
-        elif item[0] == "P":
-            particular_step(k)
+        elif item[0] == "R":
+            start(field_copies(k))
+            packed[k, me] = even_part[k, pl.ds(me * 4, 4)]
+        elif item[0] == "F":
+            finish_step(k)
         else:
-            finish_step(k)
+            particular_step(k, {"E": (0,), "O": (1,), "P": (0, 1) if has_odd(k) else (0,)}[item[0]])
 
     mode_all().wait()
+    end_all().wait()
     for u in range(NSTEP // 2):
         field_all(2 * u).wait()
         field_all(2 * u + 1).wait()
@@ -459,6 +505,8 @@
             pltpu.VMEM((units, NM, 1, 128), F32),
             pltpu.VMEM((8, 128), F32),
             pltpu.VMEM((NM, 8, 128), F32),
+            pltpu.VMEM((2, 8, 128), F32),
+            pltpu.VMEM((NM, 2, 8, 128), F32),
             dma((2,)),
             dma((NSTEP,)),
             dma((NSTEP,)),
@@ -472,12 +520,19 @@
             dma((units,)),
             dma,
             dma,
+            dma,
+            dma,
         ],
         compiler_params=pltpu.CompilerParams(
             collective_id=0, has_side_effects=True, vmem_limit_bytes=48 * 1024 * 1024
         ),
         name="solve_and_exchange",
-    )(forcing.reshape(2, NP, 16, 512), slot_wavenumber, edge_weights, inverse[0])
+    )(
+        forcing.reshape(2, NP, 16, 512),
+        pltpu.with_memory_space_constraint(slot_wavenumber, pltpu.HBM),
+        pltpu.with_memory_space_constraint(edge_weights, pltpu.HBM),
+        inverse[0],
+    )
 
 
 def solution(mesh):

time: 43.6 us -> 40.2 us (0.922)
  Pallas kernels: 40.1 us -> 38.1 us
  local copies, waits for them, and re-layouts: 3.35 us -> 2.02 us
    pallas_call x1, Pallas kernels: 40.1 us -> 38.1 us  [body(): pl.pallas_call(solve_kernel, out_shape=jax.ShapeDtypeStruct((2, 4, 2, 128...]
    unnamed x5 -> x1, local copies, waits for them, and re-layouts: 3.35 us -> 2.02 us
where the time goes in v3:
time: 40.2 us; the launch traced here: 40.1 us
  Pallas kernels  38.1 us (95%)
  local copies, waits for them, and re-layouts  2.02 us (5%)
    pallas_call x1, Pallas kernels, body(): pl.pallas_call(solve_kernel, out_shape=jax.ShapeDtypeStruct((2, 4, 2, 128...  38.1 us
    unnamed x1, local copies, waits for them, and re-layouts  2.02 us

profile of v3, /device:TPU:1, one launch (start us, length us, event | category | flops | bytes accessed | tf_op | source)
XLA Modules:
  0.0 40.1 jit_solution(261352865180769906)
XLA Ops:
  0.0 38.1 %solve_and_exchange.1 = f32[2,4,2,128,512]{4,3,2,1,0:T(8,128)S(1)} custom-call(f32[2,64,16,512]{3,2,1,0:T(8,128)} %bitcast.3, s32[8]{0:T(128)} %slot_hbm.1, f32[1,2,64]{2,1,0:T(2,128)} %edge_hbm.1, f32[2,64,64,512]{3,2,1,0:T(8,128)} %bitcast.2), custom_call_target="tpu_custom_call" | custom-call | tf_op jit(solution)/shard_map/solve_and_exchange/pallas_call | solution.py:481
  38.1 2.0 %copy.6 = f32[2,4,2,128,512]{4,3,2,1,0:T(8,128)} copy(f32[2,4,2,128,512]{4,3,2,1,0:T(8,128)S(1)} %solve_and_exchange.1) | data formatting | bytes 8388608

commit v4 on v3

--- a/solution.py
+++ b/solution.py
@@ -17,7 +17,10 @@
 PB = 8
 QB = 31
 FB = 32
-ORDER = ("S0", "E0", "R0", "S1", "O0", "S2", "P1", "F0", "F1", "S3", "P2", "F2", "S4", "P3", "F3", "S5", "P4", "F4", "S6", "P5", "F5", "S7", "P6", "F6", "P7", "F7")
+ORDER = (
+    "S0", "E0", "R0", "S1", "O0", "S2", "P1", "F0", "G0", "F1", "S3", "P2", "F2", "G2", "S4", "P3",
+    "F3", "S5", "P4", "F4", "G4", "S6", "P5", "F5", "S7", "P6", "F6", "G6", "P7", "F7",
+)
 
 
 def has_odd(k):
@@ -74,17 +77,17 @@
         for copy in copies:
             copy.start()
 
-    start(load(0))
+    barrier = pltpu.get_barrier_semaphore()
+    for other in subs:
+        pl.semaphore_signal(barrier, inc=1, device_id={"sub": other}, device_id_type=MESH)
+    for other in peers:
+        pl.semaphore_signal(barrier, inc=1, device_id={"ma": other}, device_id_type=MESH)
     small = (
         pltpu.make_async_copy(slot_hbm, slots, small_sem.at[0]),
         pltpu.make_async_copy(edge_hbm, edges, small_sem.at[1]),
     )
     start(small)
-    barrier = pltpu.get_barrier_semaphore()
-    for other in subs:
-        pl.semaphore_signal(barrier, inc=1, device_id={"sub": other}, device_id_type=MESH)
-    for other in peers:
-        pl.semaphore_signal(barrier, inc=1, device_id={"ma": other}, device_id_type=MESH)
+    start(load(0))
     for k in range(1, AHEAD):
         start(load(k))
 
@@ -302,8 +305,6 @@
             far_ends[me, 1] = above
         else:
             correct_even(k, below, above)
-        if has_odd(k):
-            correct_odd(k)
 
     def correct_even(k, below, above):
         t = STEPS[k][1]
@@ -330,7 +331,7 @@
         u = half(k)
         odd_all(k).wait()
         below, above = interface(k, 1)
-        meets = lane + (3 - t) * 128 == even_mode
+        meets = lane + t * 128 == odd_mode
 
         def block(b, _):
             for a in range(FB // 4):
@@ -338,8 +339,8 @@
                 for i in range(4):
                     p = b * FB + a * 4 + i
                     first, final = ends(k, p)
-                    other = flip_lanes((odd_part[u, p] + below * first) + above * final)
-                    odd_flip[u, p] = other
+                    other = (odd_part[u, p] + below * first) + above * final
+                    odd_flip[u, p] = flip_lanes(other)
                     value = jnp.sum(jnp.where(meets, other, 0.0), axis=1, keepdims=True)
                     last = jnp.where(lane == sublane + i * 8, value, last)
                 last_rows[u, b * (FB // 4) + a] = jnp.sum(last, axis=0, keepdims=True)
@@ -422,8 +423,8 @@
             return jnp.take_along_axis(value, pick[c], axis=0)
 
         def block(b, _):
-            for i in range(8):
-                a = b * 8 + i
+            for i in range(16):
+                a = b * 16 + i
                 mode = modes[a].astype(jnp.int32)
                 even_kept = lane + near * 128 >= mode
                 odd_at = lane + t * 128 + mode
@@ -444,7 +445,7 @@
                         out[f, p, c, rows, near * 128 : near * 128 + 128] = jnp.where(is_odd, 0.0, spread(close, c))
             return 0
 
-        lax.fori_loop(0, NM // 8, block, 0)
+        lax.fori_loop(0, NM // 16, block, 0)
 
     def greet():
         pl.semaphore_wait(barrier, len(subs) + len(peers))
@@ -461,6 +462,8 @@
             packed[k, me] = even_part[k, pl.ds(me * 4, 4)]
         elif item[0] == "F":
             finish_step(k)
+        elif item[0] == "G":
+            correct_odd(k)
         else:
             particular_step(k, {"E": (0,), "O": (1,), "P": (0, 1) if has_odd(k) else (0,)}[item[0]])
 

time: 40.2 us -> 40.2 us (level)
  no operation moved by 1% of the time
where the time goes in v4:
time: 40.2 us; the launch traced here: 40.1 us
  Pallas kernels  38.1 us (95%)
  local copies, waits for them, and re-layouts  2.02 us (5%)
    pallas_call x1, Pallas kernels, body(): pl.pallas_call(solve_kernel, out_shape=jax.ShapeDtypeStruct((2, 4, 2, 128...  38.1 us
    unnamed x1, local copies, waits for them, and re-layouts  2.02 us

profile of v4, /device:TPU:1, one launch (start us, length us, event | category | flops | bytes accessed | tf_op | source)
XLA Modules:
  0.0 40.1 jit_solution(15811142289980063482)
XLA Ops:
  0.0 38.1 %solve_and_exchange.1 = f32[2,4,2,128,512]{4,3,2,1,0:T(8,128)S(1)} custom-call(f32[2,64,16,512]{3,2,1,0:T(8,128)} %bitcast.3, s32[8]{0:T(128)} %slot_hbm.1, f32[1,2,64]{2,1,0:T(2,128)} %edge_hbm.1, f32[2,64,64,512]{3,2,1,0:T(8,128)} %bitcast.2), custom_call_target="tpu_custom_call" | custom-call | tf_op jit(solution)/shard_map/solve_and_exchange/pallas_call | solution.py:484
  38.1 2.0 %copy.6 = f32[2,4,2,128,512]{4,3,2,1,0:T(8,128)} copy(f32[2,4,2,128,512]{4,3,2,1,0:T(8,128)S(1)} %solve_and_exchange.1) | data formatting | bytes 8388608
